TPU v7x, 32 devices: a whole 2x2x4 slice. The times are simulated.
32 devices in a mesh: seq: 16 (over z, x, core), grp: 2 (over y).
Axes of the slice: x: 2, y: 2, z: 4, core: 2. Of those that a mesh axis runs over, the one named last changes fastest.
Arguments:
- out_grad: bfloat16 [2, 3456, 1024], P('grp', 'seq'), may hold values from -6 to 6
- combine_logits: float32 [2, 3456, 64], P('grp', 'seq'), may hold values from -20 to 330
- expert_out: bfloat16 [2, 64, 1024], P('grp', 'seq'), may hold values from -6 to 6
- slot_in: bfloat16 [2, 64, 1024], P('grp', 'seq'), may hold values from -6 to 6
- router: bfloat16 [64, 1024], P('seq'), may hold values from -0.1875 to 0.1875
- w_gate: bfloat16 [64, 2048, 1024], P('seq', 'grp'), may hold values from -0.1875 to 0.1875
- w_up: bfloat16 [64, 2048, 1024], P('seq', 'grp'), may hold values from -0.1875 to 0.1875
- w_down: bfloat16 [64, 2048, 1024], P('seq', 'grp'), may hold values from -0.125 to 0.125
Outputs:
- token_grad: bfloat16 [2, 3456, 1024], P('grp', 'seq')
- slot_grad: float32 [2, 64, 1024], P('grp', 'seq')
- grad_gate: bfloat16 [64, 2048, 1024], P('seq', 'grp')
- grad_up: bfloat16 [64, 2048, 1024], P('seq', 'grp')
- grad_down: bfloat16 [64, 2048, 1024], P('seq', 'grp')
All inputs are finite; a program needn't handle non-finite values.
Results may differ from a plain program's by a relative error of at most 0.028.
Values may be sent and summed in bfloat16 or wider, within the bound.
A program may use at most 128 MiB of HBM per device.

v0:
```python
import jax
import jax.numpy as jnp
from jax import lax
from jax.sharding import PartitionSpec as P


def slot_backward(inputs, out_grads, w_gate, w_up, w_down):
    gate = jnp.einsum("ged,efd->gef", inputs, w_gate, preferred_element_type=jnp.float32)
    upper = jnp.einsum("ged,efd->gef", inputs, w_up, preferred_element_type=jnp.float32)
    sig = jax.nn.sigmoid(gate)
    hidden = (gate * sig * upper).astype(jnp.bfloat16)
    hidden_grad = jnp.einsum("ged,efd->gef", out_grads, w_down, preferred_element_type=jnp.float32)
    up_grad = (hidden_grad * gate * sig).astype(jnp.bfloat16)
    gate_grad = (hidden_grad * upper * sig * (1.0 + gate * (1.0 - sig))).astype(jnp.bfloat16)
    partial_grad = jnp.einsum("gef,efd->ged", gate_grad, w_gate, preferred_element_type=jnp.float32)
    partial_grad = partial_grad + jnp.einsum(
        "gef,efd->ged", up_grad, w_up, preferred_element_type=jnp.float32
    )
    grad_gate = jnp.einsum(
        "gef,ged->efd", gate_grad, inputs, preferred_element_type=jnp.float32
    ).astype(jnp.bfloat16)
    grad_up = jnp.einsum(
        "gef,ged->efd", up_grad, inputs, preferred_element_type=jnp.float32
    ).astype(jnp.bfloat16)
    grad_down = jnp.einsum(
        "gef,ged->efd", hidden, out_grads, preferred_element_type=jnp.float32
    ).astype(jnp.bfloat16)
    return (partial_grad, grad_gate, grad_up, grad_down)


def per_device(out_grad, combine_logits, expert_out, slot_in, router, w_gate, w_up, w_down):
    grads = out_grad[0]
    probs = jax.nn.softmax(combine_logits[0], axis=-1)
    probs_bf = probs.astype(jnp.bfloat16)
    summed_cols = lax.psum_scatter(
        lax.dot_general(
            grads, probs_bf, (((0,), (0,)), ((), ())), preferred_element_type=jnp.float32
        ).astype(jnp.bfloat16),
        "seq",
        scatter_dimension=0,
        tiled=True,
    )
    owner_cols = lax.all_to_all(summed_cols, "seq", split_axis=1, concat_axis=0, tiled=True)
    slot_out = jnp.transpose(owner_cols)
    weight_grad = lax.dot_general(
        grads,
        lax.all_gather(expert_out[0], "seq", axis=0, tiled=True),
        (((1,), (1,)), ((), ())),
        preferred_element_type=jnp.float32,
    )
    centre = jnp.sum(weight_grad * probs, axis=-1, keepdims=True)
    logit_grad = (probs * (weight_grad - centre)).astype(jnp.bfloat16)
    token_sum = jnp.dot(
        logit_grad,
        lax.all_gather(router, "seq", axis=0, tiled=True),
        preferred_element_type=jnp.float32,
    )
    token_grad = token_sum.astype(jnp.bfloat16)[None]
    all_inputs, all_out = (
        lax.all_gather(slot_in, "grp", axis=0, tiled=True),
        lax.all_gather(slot_out[None], "grp", axis=0, tiled=True),
    )
    partial_grad, grad_gate, grad_up, grad_down = slot_backward(
        all_inputs, all_out, w_gate, w_up, w_down
    )
    slot_grad = lax.psum_scatter(
        partial_grad.astype(jnp.bfloat16), "grp", scatter_dimension=0, tiled=True
    ).astype(jnp.float32)
    return (token_grad, slot_grad, grad_gate, grad_up, grad_down)


def solution(mesh):
    return jax.shard_map(
        per_device,
        mesh=mesh,
        in_specs=(
            P("grp", "seq", None),
            P("grp", "seq", None),
            P("grp", "seq", None),
            P("grp", "seq", None),
            P("seq", None),
            P("seq", "grp", None),
            P("seq", "grp", None),
            P("seq", "grp", None),
        ),
        out_specs=(
            P("grp", "seq", None),
            P("grp", "seq", None),
            P("seq", "grp", None),
            P("seq", "grp", None),
            P("seq", "grp", None),
        ),
        check_vma=False,
    )
```

profile of v0, /device:TPU:0, one launch (start us, length us, event | category | flops | bytes accessed | tf_op | source)
XLA Modules:
  0.0 128.8 jit_solution(1626984013032163660)
XLA Ops:
  7.2 0.0 copy-start
  7.2 0.0 reduce-scatter.4.cloned.1.call-start
  7.2 0.9 reduce_max.9
  8.1 0.9 fusion.11
  9.0 1.0 fusion.1
  10.1 0.8 copy.38
  10.9 0.0 reduce-scatter.4.cloned.1.call-update
  10.9 5.7 %all_gather.15 = bf16[2,4,1024]{2,1,0:T(4,128)(2,1)S(1)} all-gather(bf16[1,4,1024]{2,1,0:T(4,128)(2,1)} %param.11), channel_id=1, replica_groups=mesh['seq'=16,'grp'=2] {'grp'}, dimensions={0}, use_global_device_ids=true | all-gather | bytes 24576 | tf_op jit(solution)/shard_map/all_gather | solution.py:60
  16.6 0.7 copy.29
  17.4 5.7 %convolution_bitcast_fusion = f32[2,4,1024]{2,0,1:T(2,128)S(1)} fusion(bf16[4,1024,1024]{2,1,0:T(8,128)(2,1)} %param.13, bf16[2,4,1024]{2,1,0:T(4,128)(2,1)S(1)} %all_gather.15), kind=kOutput, calls=%fused_computation.8 | convolution fusion | flops 16777216 | bytes 8437760 | tf_op jit(solution)/shard_map/ged,efd->gef/dot_general | solution.py:8
  23.1 2.3 %convolution_bitcast_fusion.1 = f32[2,4,1024]{2,0,1:T(2,128)S(1)} fusion(bf16[4,1024,1024]{2,1,0:T(8,128)(2,1)S(1)} %copy-done.1, bf16[2,4,1024]{2,1,0:T(4,128)(2,1)S(1)} %all_gather.15), kind=kOutput, calls=%fused_computation.9 | convolution fusion | flops 16777216 | bytes 8437760 | tf_op jit(solution)/shard_map/ged,efd->gef/dot_general | solution.py:9
  25.4 22.5 %all-gather.2 = bf16[16,4,1024]{2,1,0:T(4,128)(2,1)S(1)} all-gather(bf16[1,4,1024]{2,1,0:T(4,128)(2,1)S(1)} %bitcast.66), channel_id=1, replica_groups=mesh['seq'=16,'grp'=2] {'seq'}, dimensions={0}, use_global_device_ids=true | all-gather | bytes 139264 | tf_op jit(solution)/shard_map/all_gather | solution.py:55
  47.9 18.2 %all-gather = bf16[1,64,1024]{2,0,1:T(2,128)(2,1)S(1)} all-gather(bf16[1,4,1024]{2,0,1:T(2,128)(2,1)S(1)} %copy.29), channel_id=2, replica_groups=mesh['seq'=16,'grp'=2] {'seq'}, dimensions={1}, use_global_device_ids=true | all-gather | bytes 139264 | tf_op jit(solution)/shard_map/all_gather | solution.py:47
  66.2 0.3 multiply_reduce_fusion
  66.4 4.1 %reduce-scatter.4.cloned.1.call-done = bf16[64,64]{1,0:T(8,128)(2,1)} async-done(((bf16[1024,64]{1,0:T(8,128)(2,1)}), bf16[64,64]{1,0:T(8,128)(2,1)}) %reduce-scatter.4.cloned.1.call-update) | async-done | bytes 8208
  70.6 0.8 copy.39
  71.4 0.7 reshape.35
  72.1 3.7 %all-to-all-start = ((bf16[16,2,128]{2,1,0:T(2,128)(2,1)}), bf16[16,2,128]{2,1,0:T(2,128)(2,1)S(1)}, u32[]{:S(2)}, u32[]{:S(2)}) async-start(bf16[16,2,128]{2,1,0:T(2,128)(2,1)} %reshape.35), calls=%async_computation | async-start | bytes 16384 | tf_op jit(solution)/shard_map/all_to_all | solution.py:43
  75.8 1.1 fusion
  76.9 0.6 dynamic-slice
  77.5 4.7 %all-to-all-done = bf16[16,2,128]{2,1,0:T(2,128)(2,1)S(1)} async-done(((bf16[16,2,128]{2,1,0:T(2,128)(2,1)}), bf16[16,2,128]{2,1,0:T(2,128)(2,1)S(1)}, u32[]{:S(2)}, u32[]{:S(2)}) %all-to-all-start) | async-done | bytes 8224 | tf_op jit(solution)/shard_map/all_to_all | solution.py:43
  82.2 0.1 reshape.36
  82.3 0.1 all_to_all.17
  82.4 4.5 %all-gather.3 = bf16[2,4,1024]{2,1,0:T(4,128)(2,1)S(1)} all-gather(bf16[1,4,1024]{2,1,0:T(4,128)(2,1)S(1)} %bitcast.65), channel_id=3, replica_groups=mesh['seq'=16,'grp'=2] {'grp'}, dimensions={0}, use_global_device_ids=true | all-gather | bytes 24576 | tf_op jit(solution)/shard_map/all_gather | solution.py:61
  86.9 5.8 %convolution_bitcast_fusion.2 = f32[2,4,1024]{2,0,1:T(2,128)S(1)} fusion(bf16[4,1024,1024]{2,1,0:T(8,128)(2,1)} %param.15, bf16[2,4,1024]{2,1,0:T(4,128)(2,1)S(1)} %all-gather.3), kind=kOutput, calls=%fused_computation.10 | convolution fusion | flops 16777216 | bytes 8437760 | tf_op jit(solution)/shard_map/ged,efd->gef/dot_general | solution.py:12
  92.7 5.8 %convolution_convert_fusion = bf16[4,1024,1024]{2,1,0:T(8,128)(2,1)} fusion(f32[2,4,1024]{2,0,1:T(2,128)S(1)} %convolution_bitcast_fusion.1, f32[2,4,1024]{2,0,1:T(2,128)S(1)} %convolution_bitcast_fusion, bf16[2,4,1024]{2,1,0:T(4,128)(2,1)S(1)} %all-gather.3), kind=kOutput, calls=%fused_computation | convolution fusion | flops 21020672 | bytes 8470528 | tf_op jit(solution)/shard_map/gef,ged->efd/dot_general | solution.py:25
  98.5 1.2 fusion.22
  99.7 5.8 %convolution_convert_fusion.2 = bf16[4,1024,1024]{2,1,0:T(8,128)(2,1)} fusion(bf16[2,4,1024]{2,1,0:T(4,128)(2,1)S(1)} %all_gather.15, f32[2,4,1024]{2,0,1:T(2,128)S(1)} %convolution_bitcast_fusion, f32[2,4,1024]{2,0,1:T(2,128)S(1)} %convolution_bitcast_fusion.2, f32[2,4,1024]{2,0,1:T(2,128)S(1)} %convolution_bitcast_fusion.1), kind=kOutput, calls=%fused_computation.2 | convolution fusion | flops 21053440 | bytes 8503296 | tf_op jit(solution)/shard_map/gef,ged->efd/dot_general | solution.py:19
  105.6 5.8 %convolution_convert_fusion.1 = bf16[4,1024,1024]{2,1,0:T(8,128)(2,1)} fusion(bf16[2,4,1024]{2,1,0:T(4,128)(2,1)S(1)} %all_gather.15, f32[2,4,1024]{2,0,1:T(2,128)S(1)} %convolution_bitcast_fusion.2, f32[2,4,1024]{2,0,1:T(2,128)S(1)} %convolution_bitcast_fusion), kind=kOutput, calls=%fused_computation.1 | convolution fusion | flops 21020672 | bytes 8470528 | tf_op jit(solution)/shard_map/gef,ged->efd/dot_general | solution.py:22
  111.4 1.2 fusion.3
  112.6 8.1 %all-reduce = bf16[2,4,1024]{2,1,0:T(4,128)(2,1)S(1)} all-reduce(bf16[2,4,1024]{2,1,0:T(4,128)(2,1)S(1)} %copy.34), channel_id=5, replica_groups=mesh['seq'=16,'grp'=2] {'grp'}, use_global_device_ids=true, to_apply=%region_4.0.clone | all-reduce | flops 8192 | bytes 32768
  120.7 1.2 dynamic-slice_convert_fusion
  (23 shorter events, 0.1 us)
Async XLA Ops:
  7.2 1.8 %copy-start = (bf16[1,216,1024]{2,1,0:T(8,128)(2,1)S(1)}, bf16[1,216,1024]{2,1,0:T(8,128)(2,1)}, u32[]{:S(2)}) copy-start(bf16[1,216,1024]{2,1,0:T(8,128)(2,1)} %param.8) | copy-start | bytes 1327108
  7.2 63.4 %reduce-scatter.4.cloned.1.call-start = ((), (), s32[]{:S(2)}) async-start(), calls=%async_computation.2 | async-start | bytes 278528
  10.9 12.1 %copy-start.1 = (bf16[4,1024,1024]{2,1,0:T(8,128)(2,1)S(1)}, bf16[4,1024,1024]{2,1,0:T(8,128)(2,1)}, u32[]{:S(2)}) copy-start(bf16[4,1024,1024]{2,1,0:T(8,128)(2,1)} %param.14) | copy-start | bytes 25165828
  17.3 8.0 %copy-start.3 = (bf16[4,1024]{1,0:T(4,128)(2,1)S(1)}, bf16[4,1024]{1,0:T(4,128)(2,1)}, u32[]{:S(2)}) copy-start(bf16[4,1024]{1,0:T(4,128)(2,1)} %param.12) | copy-start | bytes 24580
  17.4 48.8 %copy-start.2 = (f32[1,216,64]{1,2,0:T(8,128)S(1)}, f32[1,216,64]{1,2,0:T(8,128)}, u32[]{:S(2)}) copy-start(f32[1,216,64]{1,2,0:T(8,128)} %param.9) | copy-start | bytes 165892
  17.4 59.5 %copy-start.4 = (u32[32]{0:T(128)S(1)}, u32[32]{0:T(128)}, u32[]{:S(2)}) copy-start(u32[32]{0:T(128)} %constant.17) | copy-start | bytes 388
  72.1 10.1 %all-to-all-start = ((bf16[16,2,128]{2,1,0:T(2,128)(2,1)}), bf16[16,2,128]{2,1,0:T(2,128)(2,1)S(1)}, u32[]{:S(2)}, u32[]{:S(2)}) async-start(bf16[16,2,128]{2,1,0:T(2,128)(2,1)} %reshape.35), calls=%async_computation | async-start | bytes 16384 | tf_op jit(solution)/shard_map/all_to_all | solution.py:43
  86.9 11.6 %slice-start = ((s8[8388608]{0:T(1024)(128)(4,1)}), s8[4194304]{0:T(1024)(128)(4,1)S(1)}, s32[]{:S(2)}) async-start(s8[8388608]{0:T(1024)(128)(4,1)} %bitcast.60), calls=%async_computation.3 | async-start | bytes 8388608
  92.7 5.8 %slice-start.1 = ((s8[8388608]{0:T(1024)(128)(4,1)}), s8[4194304]{0:T(1024)(128)(4,1)S(1)}, s32[]{:S(2)}) async-start(s8[8388608]{0:T(1024)(128)(4,1)} %bitcast.60), calls=%async_computation.4 | async-start | bytes 8388608
  98.5 12.8 %slice-start.2 = ((s8[8388608]{0:T(1024)(128)(4,1)}), s8[4194304]{0:T(1024)(128)(4,1)S(1)}, s32[]{:S(2)}) async-start(s8[8388608]{0:T(1024)(128)(4,1)} %bitcast.62), calls=%async_computation.5 | async-start | bytes 8388608
  99.7 11.6 %slice-start.3 = ((s8[8388608]{0:T(1024)(128)(4,1)}), s8[4194304]{0:T(1024)(128)(4,1)S(1)}, s32[]{:S(2)}) async-start(s8[8388608]{0:T(1024)(128)(4,1)} %bitcast.62), calls=%async_computation.6 | async-start | bytes 8388608
Sparse Core Ops, SparseCore 0:
  12.1 58.4 reduce-scatter.3
where the time goes:
time: 129 us
  blocking collectives  59.1 us (46%)
  matrix products  36 us (28%)
  between operations  14.1 us (11%)
  waiting for transfers between devices  8.83 us (7%)
  local copies, waits for them, and re-layouts  3.92 us (3%)
  starting transfers between devices  3.78 us (3%)
  other arithmetic  3.01 us (2%)
    all_gather x1, blocking collectives, per_device(): lax.all_gather(router, 'seq', axis=0, tiled=True)  22.5 us
    all_gather x1, blocking collectives, per_device(): lax.all_gather(expert_out[0], 'seq', axis=0, tiled=True)  18.2 us
    unnamed x1, blocking collectives  8.14 us
    dot_general x1, matrix products, slot_backward(): jnp.einsum('gef,ged->efd', hidden, out_grads, preferred_element_type=jnp....  5.82 us
    dot_general x1, matrix products, slot_backward(): jnp.einsum('gef,ged->efd', gate_grad, inputs, preferred_element_type=jnp....  5.82 us
    dot_general x1, matrix products, slot_backward(): jnp.einsum('gef,ged->efd', up_grad, inputs, preferred_element_type=jnp.fl...  5.81 us
    dot_general x1, matrix products, slot_backward(): jnp.einsum('ged,efd->gef', out_grads, w_down, preferred_element_type=jnp....  5.79 us
    dot_general x1, matrix products, slot_backward(): jnp.einsum('ged,efd->gef', inputs, w_gate, preferred_element_type=jnp.flo...  5.69 us
  transfers between devices with their start and end apart: 2, of which 2 were waited for; matrix products, arithmetic and copies ran while one was open for 8% of the time, Pallas kernels for 0%

commit v1 on v0

v1 whole, which is shorter than its diff:
```python
import functools

import jax
import jax.numpy as jnp
from jax import lax
from jax.experimental import pallas as pl
from jax.experimental.pallas import tpu as pltpu
from jax.sharding import PartitionSpec as P

MESH = pl.DeviceIdType.MESH
F32 = jnp.float32
BF16 = jnp.bfloat16
NT = (((1,), (1,)), ((), ()))
TN = (((0,), (0,)), ((), ()))


def rows_of(ref, count):
    return jnp.concatenate([ref[i].astype(F32) for i in range(count)], axis=0).astype(BF16)


def exchange_kernel(
    nseq, ngrp,
    grad_hbm, logit_hbm, eout_hbm, slot_hbm, router_hbm, gate_hbm, up_hbm, down_hbm,
    acts_ref, pair_ref, lgrad_ref, rout_ref, sgrad_ref,
    grad, logit, gate_w, up_w, down_w, part_out, part_in, pieces, slots, outs, back_out, back_in,
    load_sem, w_sem, part_ssem, part_rsem, piece_ssem, piece_rsem,
    slot_ssem, slot_rsem, out_ssem, out_rsem, back_ssem, back_rsem,
):
    s_me = lax.axis_index("seq")
    g_me = lax.axis_index("grp")
    experts = slots.shape[1]

    barrier = pltpu.get_barrier_semaphore()

    def greet_seq(d, c):
        pl.semaphore_signal(barrier, inc=1, device_id={"seq": lax.rem(s_me + d, nseq)}, device_id_type=MESH)
        return c

    def greet_grp(d, c):
        pl.semaphore_signal(barrier, inc=1, device_id={"grp": lax.rem(g_me + d, ngrp)}, device_id_type=MESH)
        return c

    lax.fori_loop(1, ngrp, greet_grp, 0)
    lax.fori_loop(1, nseq, greet_seq, 0)

    loads = [
        pltpu.make_async_copy(logit_hbm.at[0], logit, load_sem.at[0]),
        pltpu.make_async_copy(grad_hbm.at[0], grad, load_sem.at[1]),
        pltpu.make_async_copy(slot_hbm.at[0], slots.at[g_me], load_sem.at[2]),
        pltpu.make_async_copy(eout_hbm.at[0], pieces.at[s_me, 0], load_sem.at[3]),
        pltpu.make_async_copy(router_hbm, pieces.at[s_me, 1], load_sem.at[4]),
    ]
    for c in loads:
        c.start()
    w_loads = {}
    for m, (src, dst) in enumerate(((gate_hbm, gate_w), (up_hbm, up_w), (down_hbm, down_w))):
        for e in range(experts):
            w_loads[m, e] = pltpu.make_async_copy(src.at[e], dst.at[e], w_sem.at[m, e])
    for e in range(experts):
        w_loads[0, e].start()
        w_loads[1, e].start()
    for e in range(experts):
        w_loads[2, e].start()

    def part_copy(d):
        to = lax.rem(s_me + d, nseq)
        return pltpu.make_async_remote_copy(
            src_ref=part_out.at[to], dst_ref=part_in.at[s_me],
            send_sem=part_ssem.at[to], recv_sem=part_rsem.at[s_me],
            device_id={"seq": to}, device_id_type=MESH)

    def piece_copy(d):
        to = lax.rem(s_me + d, nseq)
        return pltpu.make_async_remote_copy(
            src_ref=pieces.at[s_me], dst_ref=pieces.at[s_me],
            send_sem=piece_ssem.at[to], recv_sem=piece_rsem.at[s_me],
            device_id={"seq": to}, device_id_type=MESH)

    def grp_copy(d, src, dst, ssem, rsem):
        to = lax.rem(g_me + d, ngrp)
        return pltpu.make_async_remote_copy(
            src_ref=src.at[to] if src is not dst else src.at[g_me], dst_ref=dst.at[g_me],
            send_sem=ssem.at[to], recv_sem=rsem.at[g_me],
            device_id={"grp": to}, device_id_type=MESH)

    def seq_arrived(d, buf, rsem, ssem):
        at = lax.rem(s_me + d, nseq)
        pltpu.make_async_remote_copy(
            src_ref=buf.at[at], dst_ref=buf.at[at], send_sem=ssem.at[at], recv_sem=rsem.at[at],
            device_id={"seq": at}, device_id_type=MESH).wait_recv()

    def grp_arrived(d, buf, rsem, ssem):
        at = lax.rem(g_me + d, ngrp)
        pltpu.make_async_remote_copy(
            src_ref=buf.at[at], dst_ref=buf.at[at], send_sem=ssem.at[at], recv_sem=rsem.at[at],
            device_id={"grp": at}, device_id_type=MESH).wait_recv()

    def each(low, high, fn):
        def step(d, c):
            fn(d)
            return c
        lax.fori_loop(low, high, step, 0)

    loads[0].wait()
    z = logit[...]
    z = jnp.exp(z - jnp.max(z, axis=-1, keepdims=True))
    probs = z / jnp.sum(z, axis=-1, keepdims=True)
    logit[...] = probs
    loads[1].wait()
    share = lax.dot_general(probs.astype(BF16), grad[...], TN, preferred_element_type=F32)
    for j in range(nseq):
        part_out[j] = share[j * experts:(j + 1) * experts].astype(BF16)
    part_in[s_me] = part_out[s_me]
    for c in loads[2:]:
        c.wait()

    pl.semaphore_wait(barrier, (nseq - 1) + (ngrp - 1))
    each(1, ngrp, lambda d: grp_copy(d, slots, slots, slot_ssem, slot_rsem).start())
    each(1, nseq, lambda d: part_copy(d).start())
    each(1, nseq, lambda d: piece_copy(d).start())

    rows = ngrp * experts
    width = gate_w.shape[1]
    own = lax.rem(lax.broadcasted_iota(jnp.int32, (rows, width), 0), experts)

    each(1, ngrp, lambda d: grp_arrived(d, slots, slot_rsem, slot_ssem))
    x = rows_of(slots, ngrp)
    pair_ref[0] = x

    gate = jnp.zeros((rows, width), F32)
    upper = jnp.zeros((rows, width), F32)

    def project(e, gate, upper):
        w_loads[0, e].wait()
        gate = jnp.where(own == e, lax.dot_general(x, gate_w[e], NT, preferred_element_type=F32), gate)
        w_loads[1, e].wait()
        upper = jnp.where(own == e, lax.dot_general(x, up_w[e], NT, preferred_element_type=F32), upper)
        return gate, upper

    early = experts // 2
    for e in range(early):
        gate, upper = project(e, gate, upper)

    each(1, nseq, lambda d: seq_arrived(d, part_in, part_rsem, part_ssem))
    outs[g_me] = jnp.sum(part_in[...].astype(F32), axis=0).astype(BF16)
    each(1, ngrp, lambda d: grp_copy(d, outs, outs, out_ssem, out_rsem).start())

    for e in range(early, experts):
        gate, upper = project(e, gate, upper)
    sig = jax.nn.sigmoid(gate)
    act = gate * sig
    acts_ref[2] = (act * upper).astype(BF16)

    each(1, ngrp, lambda d: grp_arrived(d, outs, out_rsem, out_ssem))
    so = rows_of(outs, ngrp)
    pair_ref[1] = so
    hgrad = jnp.zeros((rows, width), F32)
    for e in range(experts):
        w_loads[2, e].wait()
        hgrad = jnp.where(own == e, lax.dot_general(so, down_w[e], NT, preferred_element_type=F32), hgrad)
    up_grad = (hgrad * gate * sig).astype(BF16)
    gate_grad = (hgrad * upper * sig * (1.0 + gate * (1.0 - sig))).astype(BF16)
    acts_ref[0] = gate_grad
    acts_ref[1] = up_grad

    gate_f, up_f = gate_grad.astype(F32), up_grad.astype(F32)
    total = jnp.zeros((rows, x.shape[1]), F32)
    for e in range(experts):
        total += jnp.dot(jnp.where(own == e, gate_f, 0.0).astype(BF16), gate_w[e], preferred_element_type=F32)
        total += jnp.dot(jnp.where(own == e, up_f, 0.0).astype(BF16), up_w[e], preferred_element_type=F32)
    for g in range(ngrp):
        back_out[g] = total[g * experts:(g + 1) * experts].astype(BF16)
    back_in[g_me] = back_out[g_me]
    each(1, ngrp, lambda d: grp_copy(d, back_out, back_in, back_ssem, back_rsem).start())

    each(1, nseq, lambda d: seq_arrived(d, pieces, piece_rsem, piece_ssem))
    eout = rows_of(pieces.at[:, 0], nseq)
    rout_ref[...] = rows_of(pieces.at[:, 1], nseq)
    wgrad = lax.dot_general(grad[...], eout, NT, preferred_element_type=F32)
    p = logit[...]
    centre = jnp.sum(wgrad * p, axis=-1, keepdims=True)
    lgrad_ref[...] = (p * (wgrad - centre)).astype(BF16)

    each(1, ngrp, lambda d: grp_arrived(d, back_in, back_rsem, back_ssem))
    sgrad_ref[...] = jnp.sum(back_in[...].astype(F32), axis=0)

    each(1, nseq, lambda d: part_copy(d).wait_send())
    each(1, nseq, lambda d: piece_copy(d).wait_send())
    each(1, ngrp, lambda d: grp_copy(d, slots, slots, slot_ssem, slot_rsem).wait_send())
    each(1, ngrp, lambda d: grp_copy(d, outs, outs, out_ssem, out_rsem).wait_send())
    each(1, ngrp, lambda d: grp_copy(d, back_out, back_in, back_ssem, back_rsem).wait_send())


def write_kernel(experts, acts_ref, pair_ref, lgrad_ref, rout_ref, sgrad_in, tgrad_ref, sgrad_ref, gg_ref, gu_ref, gd_ref):
    e = pl.program_id(0)

    @pl.when((e == 0) & (pl.program_id(1) == 0))
    def _():
        tgrad_ref[0] = jnp.dot(lgrad_ref[...], rout_ref[...], preferred_element_type=F32).astype(BF16)
        sgrad_ref[0] = sgrad_in[...]

    shape = acts_ref.shape[1:]
    own = lax.rem(lax.broadcasted_iota(jnp.int32, shape, 0), experts) == e
    for k, (src, out) in enumerate(((0, gg_ref), (0, gu_ref), (1, gd_ref))):
        a = jnp.where(own, acts_ref[k].astype(F32), 0.0).astype(BF16)
        out[0] = lax.dot_general(a, pair_ref[src], TN, preferred_element_type=F32).astype(BF16)


def per_device(nseq, ngrp, out_grad, combine_logits, expert_out, slot_in, router, w_gate, w_up, w_down):
    _, tokens, dim = out_grad.shape
    total_experts = combine_logits.shape[2]
    experts, width, _ = w_gate.shape
    rows = ngrp * experts
    DMA = pltpu.SemaphoreType.DMA
    anyspec = pl.BlockSpec(memory_space=pl.ANY)
    vspec = pl.BlockSpec(memory_space=pltpu.VMEM)
    acts, pair, lgrad, rout, sgrad = pl.pallas_call(
        functools.partial(exchange_kernel, nseq, ngrp),
        out_shape=(
            jax.ShapeDtypeStruct((3, rows, width), BF16),
            jax.ShapeDtypeStruct((2, rows, dim), BF16),
            jax.ShapeDtypeStruct((tokens, total_experts), BF16),
            jax.ShapeDtypeStruct((total_experts, dim), BF16),
            jax.ShapeDtypeStruct((experts, dim), F32),
        ),
        in_specs=[anyspec] * 8,
        out_specs=(vspec,) * 5,
        scratch_shapes=[
            pltpu.VMEM((tokens, dim), BF16),
            pltpu.VMEM((tokens, total_experts), F32),
            pltpu.VMEM((experts, width, dim), BF16),
            pltpu.VMEM((experts, width, dim), BF16),
            pltpu.VMEM((experts, width, dim), BF16),
            pltpu.VMEM((nseq, experts, dim), BF16),
            pltpu.VMEM((nseq, experts, dim), BF16),
            pltpu.VMEM((nseq, 2, experts, dim), BF16),
            pltpu.VMEM((ngrp, experts, dim), BF16),
            pltpu.VMEM((ngrp, experts, dim), BF16),
            pltpu.VMEM((ngrp, experts, dim), BF16),
            pltpu.VMEM((ngrp, experts, dim), BF16),
            DMA((5,)), DMA((3, experts)),
            DMA((nseq,)), DMA((nseq,)), DMA((nseq,)), DMA((nseq,)),
            DMA((ngrp,)), DMA((ngrp,)), DMA((ngrp,)), DMA((ngrp,)), DMA((ngrp,)), DMA((ngrp,)),
        ],
        compiler_params=pltpu.CompilerParams(
            collective_id=0, has_side_effects=True, vmem_limit_bytes=48 * 1024 * 1024),
        name="exchange",
    )(out_grad, combine_logits, expert_out, slot_in, router, w_gate, w_up, w_down)

    cut = 256 if width % 256 == 0 else width
    whole = lambda *shape: pl.BlockSpec(shape, lambda e, j: (0,) * len(shape))
    big = pl.BlockSpec((1, cut, dim), lambda e, j: (e, j, 0))
    return pl.pallas_call(
        functools.partial(write_kernel, experts),
        grid=(experts, width // cut),
        out_shape=(
            jax.ShapeDtypeStruct((1, tokens, dim), BF16),
            jax.ShapeDtypeStruct((1, experts, dim), F32),
        ) + (jax.ShapeDtypeStruct((experts, width, dim), BF16),) * 3,
        in_specs=[
            pl.BlockSpec((3, rows, cut), lambda e, j: (0, 0, j)),
            whole(2, rows, dim), whole(tokens, total_experts), whole(total_experts, dim), whole(experts, dim),
        ],
        out_specs=(whole(1, tokens, dim), whole(1, experts, dim), big, big, big),
        compiler_params=pltpu.CompilerParams(vmem_limit_bytes=24 * 1024 * 1024),
        name="write",
    )(acts, pair, lgrad, rout, sgrad)


def solution(mesh):
    return jax.shard_map(
        functools.partial(per_device, mesh.shape["seq"], mesh.shape["grp"]),
        mesh=mesh,
        in_specs=(
            P("grp", "seq", None),
            P("grp", "seq", None),
            P("grp", "seq", None),
            P("grp", "seq", None),
            P("seq", None),
            P("seq", "grp", None),
            P("seq", "grp", None),
            P("seq", "grp", None),
        ),
        out_specs=(
            P("grp", "seq", None),
            P("grp", "seq", None),
            P("seq", "grp", None),
            P("seq", "grp", None),
            P("seq", "grp", None),
        ),
        check_vma=False,
    )
```

time: 129 us -> 41.9 us (0.32)
  blocking collectives: 59.1 us -> 0 us
  Pallas kernels: 0 us -> 36.9 us
  matrix products: 36 us -> 0 us
  between operations: 14.1 us -> 0.65 us
  waiting for transfers between devices: 8.83 us -> 0 us
  starting transfers between devices: 3.78 us -> 0 us
  other arithmetic: 3.01 us -> 0 us
    all_gather x4 -> x0, blocking collectives: 51 us -> none  [the longest x1 22.5 us: per_device(): lax.all_gather(router, 'seq', axis=0, tiled=True)]
    pallas_call x0 -> x2, Pallas kernels: none -> 36.9 us  [the longest x1 23.2 us: per_device(): pl.pallas_call(functools.partial(exchange_kernel, nseq, ngrp), out_shape=...]
    dot_general x11 -> x0, matrix products: 36 us -> none  [the longest x1 5.82 us: slot_backward(): jnp.einsum('gef,ged->efd', hidden, out_grads, preferred_element_type=jnp....]
    unnamed x1 -> x0, blocking collectives: 8.14 us -> none
    all_to_all x1 -> x0, waiting for transfers between devices: 4.69 us -> none  [per_device(): lax.all_to_all(summed_cols, 'seq', split_axis=1, concat_axis=0, tiled=True)]
    unnamed x2 -> x0, waiting for transfers between devices: 4.14 us -> none
    all_to_all x1 -> x0, starting transfers between devices: 3.74 us -> none  [per_device(): lax.all_to_all(summed_cols, 'seq', split_axis=1, concat_axis=0, tiled=True)]
    unnamed x25 -> x9, local copies, waits for them, and re-layouts: 3.81 us -> 4.03 us
  transfers between devices with their start and end apart: 2 -> 0, of which waited for: 2 -> 0; matrix products, arithmetic and copies ran while one was open for 8% -> 0% of each run, Pallas kernels for 0% -> 0%
where the time goes in v1:
time: 41.9 us; the launch traced here: 41.6 us
  Pallas kernels  36.9 us (88%)
  local copies, waits for them, and re-layouts  4.03 us (10%)
  between operations  0.65 us (2%)
    pallas_call x1, Pallas kernels, per_device(): pl.pallas_call(functools.partial(exchange_kernel, nseq, ngrp), out_shape=...  23.2 us
    pallas_call x1, Pallas kernels, per_device(): pl.pallas_call(functools.partial(write_kernel, experts), grid=(experts, w...  13.7 us
    unnamed x9, local copies, waits for them, and re-layouts  4.03 us

profile of v1, /device:TPU:0, one launch (start us, length us, event | category | flops | bytes accessed | tf_op | source)
XLA Modules:
  0.0 41.6 jit_solution(15449964133387881044)
XLA Ops:
  0.6 0.9 %copy.13.logit_hbm = f32[1,216,64]{2,1,0:T(8,128)S(1)} copy(f32[1,216,64]{1,2,0:T(8,128)} %param.9) | data formatting | bytes 110592 | tf_op args[1]
  1.6 0.0 copy-start
  1.6 1.0 %copy-done = bf16[1,216,1024]{2,1,0:T(8,128)(2,1)S(1)} copy-done((bf16[1,216,1024]{2,1,0:T(8,128)(2,1)S(1)}, bf16[1,216,1024]{2,1,0:T(8,128)(2,1)}, u32[]{:S(2)}) %copy-start) | copy-done | bytes 442392
  2.6 0.0 copy-start.1
  2.6 0.7 %copy-done.1 = bf16[1,4,1024]{2,1,0:T(4,128)(2,1)S(1)} copy-done((bf16[1,4,1024]{2,1,0:T(4,128)(2,1)S(1)}, bf16[1,4,1024]{2,1,0:T(4,128)(2,1)}, u32[]{:S(2)}) %copy-start.1) | copy-done | bytes 8216
  3.3 0.0 copy-start.2
  3.3 0.7 %copy-done.2 = bf16[1,4,1024]{2,1,0:T(4,128)(2,1)S(1)} copy-done((bf16[1,4,1024]{2,1,0:T(4,128)(2,1)S(1)}, bf16[1,4,1024]{2,1,0:T(4,128)(2,1)}, u32[]{:S(2)}) %copy-start.2) | copy-done | bytes 8216
  4.0 0.0 copy-start.3
  4.0 0.7 %copy-done.3 = bf16[4,1024]{1,0:T(4,128)(2,1)S(1)} copy-done((bf16[4,1024]{1,0:T(4,128)(2,1)S(1)}, bf16[4,1024]{1,0:T(4,128)(2,1)}, u32[]{:S(2)}) %copy-start.3) | copy-done | bytes 8216
  4.7 23.2 %exchange.1 = (bf16[3,8,1024]{2,1,0:T(8,128)(2,1)S(1)}, bf16[2,8,1024]{2,1,0:T(8,128)(2,1)S(1)}, bf16[216,64]{1,0:T(8,128)(2,1)S(1)}, bf16[64,1024]{1,0:T(8,128)(2,1)S(1)}, f32[4,1024]{1,0:T(4,128)S(1)}) custom-call(bf16[1,216,1024]{2,1,0:T(8,128)(2,1)S(1)} %copy-done, f32[1,216,64]{2,1,0:T(8,128)S(1)} %copy.13.logit_hbm, bf16[1,4,1024]{2,1,0:T(4,128)(2,1)S(1)} %copy-done.1, ...), custom_call_target="tpu_custom_call" | custom-call | tf_op jit(solution)/shard_map/exchange/pallas_call | solution.py:217
  27.9 13.7 %write.1 = (bf16[1,216,1024]{2,1,0:T(8,128)(2,1)}, f32[1,4,1024]{2,1,0:T(4,128)}, bf16[4,1024,1024]{2,1,0:T(8,128)(2,1)}, bf16[4,1024,1024]{2,1,0:T(8,128)(2,1)}, bf16[4,1024,1024]{2,1,0:T(8,128)(2,1)}) custom-call(bf16[3,8,1024]{2,1,0:T(8,128)(2,1)S(1)} %get-tuple-element.10.acts_ref, bf16[2,8,1024]{2,1,0:T(8,128)(2,1)S(1)} %get-tuple-element.11.pair_ref, ...), custom_call_target="tpu_custom_call" | custom-call | tf_op jit(solution)/shard_map/write/pallas_call | solution.py:253
Async XLA Ops:
  1.6 1.0 %copy-start = (bf16[1,216,1024]{2,1,0:T(8,128)(2,1)S(1)}, bf16[1,216,1024]{2,1,0:T(8,128)(2,1)}, u32[]{:S(2)}) copy-start(bf16[1,216,1024]{2,1,0:T(8,128)(2,1)} %grad_hbm.1) | copy-start | bytes 1327108
  2.6 0.7 %copy-start.1 = (bf16[1,4,1024]{2,1,0:T(4,128)(2,1)S(1)}, bf16[1,4,1024]{2,1,0:T(4,128)(2,1)}, u32[]{:S(2)}) copy-start(bf16[1,4,1024]{2,1,0:T(4,128)(2,1)} %eout_hbm.1) | copy-start | bytes 24580
  3.3 0.7 %copy-start.2 = (bf16[1,4,1024]{2,1,0:T(4,128)(2,1)S(1)}, bf16[1,4,1024]{2,1,0:T(4,128)(2,1)}, u32[]{:S(2)}) copy-start(bf16[1,4,1024]{2,1,0:T(4,128)(2,1)} %slot_hbm.1) | copy-start | bytes 24580
  4.0 0.7 %copy-start.3 = (bf16[4,1024]{1,0:T(4,128)(2,1)S(1)}, bf16[4,1024]{1,0:T(4,128)(2,1)}, u32[]{:S(2)}) copy-start(bf16[4,1024]{1,0:T(4,128)(2,1)} %router_hbm.1) | copy-start | bytes 24580

commit v2 on v1

--- a/solution.py
+++ b/solution.py
@@ -44,7 +44,7 @@
     lax.fori_loop(1, nseq, greet_seq, 0)
 
     loads = [
-        pltpu.make_async_copy(logit_hbm.at[0], logit, load_sem.at[0]),
+        pltpu.make_async_copy(logit_hbm, logit, load_sem.at[0]),
         pltpu.make_async_copy(grad_hbm.at[0], grad, load_sem.at[1]),
         pltpu.make_async_copy(slot_hbm.at[0], slots.at[g_me], load_sem.at[2]),
         pltpu.make_async_copy(eout_hbm.at[0], pieces.at[s_me, 0], load_sem.at[3]),
@@ -103,11 +103,11 @@
 
     loads[0].wait()
     z = logit[...]
-    z = jnp.exp(z - jnp.max(z, axis=-1, keepdims=True))
-    probs = z / jnp.sum(z, axis=-1, keepdims=True)
+    z = jnp.exp(z - jnp.max(z, axis=0, keepdims=True))
+    probs = z / jnp.sum(z, axis=0, keepdims=True)
     logit[...] = probs
     loads[1].wait()
-    share = lax.dot_general(probs.astype(BF16), grad[...], TN, preferred_element_type=F32)
+    share = jnp.dot(probs.astype(BF16), grad[...], preferred_element_type=F32)
     for j in range(nseq):
         part_out[j] = share[j * experts:(j + 1) * experts].astype(BF16)
     part_in[s_me] = part_out[s_me]
@@ -176,9 +176,9 @@
     each(1, nseq, lambda d: seq_arrived(d, pieces, piece_rsem, piece_ssem))
     eout = rows_of(pieces.at[:, 0], nseq)
     rout_ref[...] = rows_of(pieces.at[:, 1], nseq)
-    wgrad = lax.dot_general(grad[...], eout, NT, preferred_element_type=F32)
+    wgrad = lax.dot_general(eout, grad[...], NT, preferred_element_type=F32)
     p = logit[...]
-    centre = jnp.sum(wgrad * p, axis=-1, keepdims=True)
+    centre = jnp.sum(wgrad * p, axis=0, keepdims=True)
     lgrad_ref[...] = (p * (wgrad - centre)).astype(BF16)
 
     each(1, ngrp, lambda d: grp_arrived(d, back_in, back_rsem, back_ssem))
@@ -191,19 +191,44 @@
     each(1, ngrp, lambda d: grp_copy(d, back_out, back_in, back_ssem, back_rsem).wait_send())
 
 
-def write_kernel(experts, acts_ref, pair_ref, lgrad_ref, rout_ref, sgrad_in, tgrad_ref, sgrad_ref, gg_ref, gu_ref, gd_ref):
-    e = pl.program_id(0)
-
-    @pl.when((e == 0) & (pl.program_id(1) == 0))
-    def _():
-        tgrad_ref[0] = jnp.dot(lgrad_ref[...], rout_ref[...], preferred_element_type=F32).astype(BF16)
-        sgrad_ref[0] = sgrad_in[...]
-
-    shape = acts_ref.shape[1:]
-    own = lax.rem(lax.broadcasted_iota(jnp.int32, shape, 0), experts) == e
-    for k, (src, out) in enumerate(((0, gg_ref), (0, gu_ref), (1, gd_ref))):
-        a = jnp.where(own, acts_ref[k].astype(F32), 0.0).astype(BF16)
-        out[0] = lax.dot_general(a, pair_ref[src], TN, preferred_element_type=F32).astype(BF16)
+def write_kernel(
+    experts, cut,
+    acts_ref, pair_ref, lgrad_ref, rout_ref, sgrad_in,
+    tgrad_hbm, sgrad_hbm, gg_hbm, gu_hbm, gd_hbm,
+    staged, tokens, sem, small_sem,
+):
+    outs = (gg_hbm, gu_hbm, gd_hbm)
+    width = acts_ref.shape[2]
+    own = lax.rem(lax.broadcasted_iota(jnp.int32, acts_ref.shape[1:], 0), experts)
+
+    def chunk(k, e, j):
+        at = pl.ds(j * cut, cut)
+        return pltpu.make_async_copy(staged.at[k, e, at], outs[k].at[e, at], sem.at[k, e, j])
+
+    def expert(e, c):
+        for k, src in enumerate((0, 0, 1)):
+            a = jnp.where(own == e, acts_ref[k].astype(F32), 0.0).astype(BF16)
+            for j in range(width // cut):
+                at = slice(j * cut, (j + 1) * cut)
+                staged[k, e, at] = lax.dot_general(
+                    a[:, at], pair_ref[src], TN, preferred_element_type=F32).astype(BF16)
+                chunk(k, e, j).start()
+        return c
+
+    lax.fori_loop(0, experts, expert, 0)
+    tokens[...] = lax.dot_general(lgrad_ref[...], rout_ref[...], TN, preferred_element_type=F32).astype(BF16)
+    small = [
+        pltpu.make_async_copy(tokens, tgrad_hbm.at[0], small_sem.at[0]),
+        pltpu.make_async_copy(sgrad_in, sgrad_hbm.at[0], small_sem.at[1]),
+    ]
+    for c in small:
+        c.start()
+    for e in range(experts):
+        for k in range(3):
+            for j in range(width // cut):
+                chunk(k, e, j).wait()
+    for c in small:
+        c.wait()
 
 
 def per_device(nseq, ngrp, out_grad, combine_logits, expert_out, slot_in, router, w_gate, w_up, w_down):
@@ -212,14 +237,14 @@
     experts, width, _ = w_gate.shape
     rows = ngrp * experts
     DMA = pltpu.SemaphoreType.DMA
-    anyspec = pl.BlockSpec(memory_space=pl.ANY)
+    anyspec = pl.BlockSpec(memory_space=pltpu.HBM)
     vspec = pl.BlockSpec(memory_space=pltpu.VMEM)
     acts, pair, lgrad, rout, sgrad = pl.pallas_call(
         functools.partial(exchange_kernel, nseq, ngrp),
         out_shape=(
             jax.ShapeDtypeStruct((3, rows, width), BF16),
             jax.ShapeDtypeStruct((2, rows, dim), BF16),
-            jax.ShapeDtypeStruct((tokens, total_experts), BF16),
+            jax.ShapeDtypeStruct((total_experts, tokens), BF16),
             jax.ShapeDtypeStruct((total_experts, dim), BF16),
             jax.ShapeDtypeStruct((experts, dim), F32),
         ),
@@ -227,7 +252,7 @@
         out_specs=(vspec,) * 5,
         scratch_shapes=[
             pltpu.VMEM((tokens, dim), BF16),
-            pltpu.VMEM((tokens, total_experts), F32),
+            pltpu.VMEM((total_experts, tokens), F32),
             pltpu.VMEM((experts, width, dim), BF16),
             pltpu.VMEM((experts, width, dim), BF16),
             pltpu.VMEM((experts, width, dim), BF16),
@@ -245,24 +270,25 @@
         compiler_params=pltpu.CompilerParams(
             collective_id=0, has_side_effects=True, vmem_limit_bytes=48 * 1024 * 1024),
         name="exchange",
-    )(out_grad, combine_logits, expert_out, slot_in, router, w_gate, w_up, w_down)
+    )(*(pltpu.with_memory_space_constraint(a, pltpu.HBM) for a in (
+        out_grad, jnp.transpose(combine_logits[0]), expert_out, slot_in, router, w_gate, w_up, w_down)))
 
     cut = 256 if width % 256 == 0 else width
-    whole = lambda *shape: pl.BlockSpec(shape, lambda e, j: (0,) * len(shape))
-    big = pl.BlockSpec((1, cut, dim), lambda e, j: (e, j, 0))
     return pl.pallas_call(
-        functools.partial(write_kernel, experts),
-        grid=(experts, width // cut),
+        functools.partial(write_kernel, experts, cut),
         out_shape=(
             jax.ShapeDtypeStruct((1, tokens, dim), BF16),
             jax.ShapeDtypeStruct((1, experts, dim), F32),
         ) + (jax.ShapeDtypeStruct((experts, width, dim), BF16),) * 3,
-        in_specs=[
-            pl.BlockSpec((3, rows, cut), lambda e, j: (0, 0, j)),
-            whole(2, rows, dim), whole(tokens, total_experts), whole(total_experts, dim), whole(experts, dim),
+        in_specs=[vspec] * 5,
+        out_specs=(pl.BlockSpec(memory_space=pltpu.HBM),) * 5,
+        scratch_shapes=[
+            pltpu.VMEM((3, experts, width, dim), BF16),
+            pltpu.VMEM((tokens, dim), BF16),
+            DMA((3, experts, width // cut)),
+            DMA((2,)),
         ],
-        out_specs=(whole(1, tokens, dim), whole(1, experts, dim), big, big, big),
-        compiler_params=pltpu.CompilerParams(vmem_limit_bytes=24 * 1024 * 1024),
+        compiler_params=pltpu.CompilerParams(vmem_limit_bytes=40 * 1024 * 1024),
         name="write",
     )(acts, pair, lgrad, rout, sgrad)
 

time: 41.9 us -> 37.8 us (0.902)
  local copies, waits for them, and re-layouts: 4.03 us -> 0 us
    pallas_call x1, Pallas kernels: 13.7 us -> 9.2 us  [per_device(): pl.pallas_call(functools.partial(write_kernel, experts, cut), out_shape=(...]
    pallas_call x1, Pallas kernels: 23.2 us -> 27.3 us  [per_device(): pl.pallas_call(functools.partial(exchange_kernel, nseq, ngrp), out_shape=...]
    unnamed x9 -> x0, local copies, waits for them, and re-layouts: 4.03 us -> none
where the time goes in v2:
time: 37.8 us; the launch traced here: 37.1 us
  Pallas kernels  36.5 us (97%)
  between operations  0.64 us (2%)
    pallas_call x1, Pallas kernels, per_device(): pl.pallas_call(functools.partial(exchange_kernel, nseq, ngrp), out_shape=...  27.3 us
    pallas_call x1, Pallas kernels, per_device(): pl.pallas_call(functools.partial(write_kernel, experts, cut), out_shape=(...  9.2 us

profile of v2, /device:TPU:0, one launch (start us, length us, event | category | flops | bytes accessed | tf_op | source)
XLA Modules:
  0.0 37.1 jit_solution(5124203022002705368)
XLA Ops:
  0.6 27.3 %exchange.1 = (bf16[3,8,1024]{2,1,0:T(8,128)(2,1)S(1)}, bf16[2,8,1024]{2,1,0:T(8,128)(2,1)S(1)}, bf16[64,216]{1,0:T(8,128)(2,1)S(1)}, bf16[64,1024]{1,0:T(8,128)(2,1)S(1)}, f32[4,1024]{1,0:T(4,128)S(1)}) custom-call(bf16[1,216,1024]{2,1,0:T(8,128)(2,1)} %grad_hbm.1, f32[64,216]{1,0:T(8,128)} %bitcast.3, bf16[1,4,1024]{2,1,0:T(4,128)(2,1)} %eout_hbm.1, ...), custom_call_target="tpu_custom_call" | custom-call | tf_op jit(solution)/shard_map/exchange/pallas_call | solution.py:242
  27.9 9.2 %write.1 = (bf16[1,216,1024]{2,1,0:T(8,128)(2,1)}, f32[1,4,1024]{2,1,0:T(4,128)}, bf16[4,1024,1024]{2,1,0:T(8,128)(2,1)}, bf16[4,1024,1024]{2,1,0:T(8,128)(2,1)}, bf16[4,1024,1024]{2,1,0:T(8,128)(2,1)}) custom-call(bf16[3,8,1024]{2,1,0:T(8,128)(2,1)S(1)} %get-tuple-element.10.acts_ref, bf16[2,8,1024]{2,1,0:T(8,128)(2,1)S(1)} %get-tuple-element.11.pair_ref, ...), custom_call_target="tpu_custom_call" | custom-call | tf_op jit(solution)/shard_map/write/pallas_call | solution.py:277
